TPU v7x, 32 devices: a whole 2x2x4 slice. The times are simulated.
32 devices in a mesh: sub: 2 (over y), row: 4 (over x, core), col: 4 (over z).
Axes of the slice: x: 2, y: 2, z: 4, core: 2. Of those that a mesh axis runs over, the one named last changes fastest.
Arguments:
- visibility: bfloat16 [2, 16, 512, 4096], P(None, 'sub', 'row', 'col'), may hold values from -13 to 13
- sky_model: bfloat16 [2, 16, 512, 4096], P(None, 'sub', 'row', 'col'), may hold values from -4 to 4, as said below
- antenna_flags: int32 [2, 512], P('sub'), may hold values 0 or 1
- gains_init: float32 [2, 16, 512], P(None, 'sub'), may hold values from -0.5 to 1.5
Outputs:
- gains: float32 [2, 16, 512], P(None, 'sub')
Inputs may be any that keep to these rules, and one draw needn't show every extreme that they name: `sky_model`: model visibility parts lie between -4 and 4.
All inputs are finite; a program needn't handle non-finite values.
Results may differ from a plain program's by a relative error of at most 0.0003.
Values sent between devices are 32-bit elements.
A program may use at most 64 MiB of HBM per device.

v0:
```python
import jax
import jax.numpy as jnp
from jax import lax
from jax.sharding import PartitionSpec as P

TIMES = 8
ITERS = 3


def subband_total(values):
    return lax.psum(values, "sub")


def update_gains(summed, previous):
    denominator = summed[:, 2, :] + 1.0
    quotient = jnp.stack([summed[:, 0, :] / denominator, summed[:, 1, :] / denominator], axis=0)
    updated = 0.5 * (quotient + previous)
    chan_mean = jnp.sum(updated, axis=1) / updated.shape[1]
    overall = subband_total(chan_mean) / lax.axis_size("sub")
    return updated + 0.5 * (overall - chan_mean)[:, None, :]


def time_total(values, selector):
    return jnp.einsum(
        "crk,kq->crq",
        values,
        selector,
        precision=lax.Precision.HIGHEST,
        preferred_element_type=jnp.float32,
    )


def contract(matrix, vector):
    return jnp.einsum("cpq,cq->cp", matrix, vector, precision=lax.Precision.HIGHEST)


def body(visibility, sky_model, antenna_flags, gains_init):
    block_rows = visibility.shape[2]
    wide_cols = visibility.shape[3]
    block_cols = wide_cols // TIMES
    row_at = lax.axis_index("row") * block_rows
    col_at = lax.axis_index("col") * block_cols
    flag_value = antenna_flags[0].astype(jnp.float32)
    row_flag = lax.dynamic_slice_in_dim(flag_value, row_at, block_rows)
    col_flag = lax.dynamic_slice_in_dim(flag_value, col_at, block_cols)
    row_ids = row_at + lax.iota(jnp.int32, block_rows)
    col_ids = col_at + lax.iota(jnp.int32, block_cols)
    weight = (
        row_flag[:, None]
        * col_flag[None, :]
        * (row_ids[:, None] != col_ids[None, :]).astype(jnp.float32)
    )
    selector = (
        lax.iota(jnp.int32, wide_cols)[:, None] // TIMES == lax.iota(jnp.int32, block_cols)[None, :]
    ).astype(jnp.float32)
    vis_re = visibility[0].astype(jnp.float32)
    vis_im = visibility[1].astype(jnp.float32)
    mod_re = sky_model[0].astype(jnp.float32)
    mod_im = sky_model[1].astype(jnp.float32)
    cross_re = time_total(vis_re * mod_re + vis_im * mod_im, selector) * weight
    cross_im = time_total(vis_im * mod_re - vis_re * mod_im, selector) * weight
    power_sum = time_total(mod_re * mod_re + mod_im * mod_im, selector) * weight
    gain_values = gains_init
    for step_index in range(ITERS):
        col_gains = lax.dynamic_slice_in_dim(gain_values, col_at, block_cols, 2)
        gain_re = col_gains[0]
        gain_im = col_gains[1]
        num_re = contract(cross_re, gain_re) - contract(cross_im, gain_im)
        num_im = contract(cross_re, gain_im) + contract(cross_im, gain_re)
        denominator = contract(power_sum, gain_re * gain_re + gain_im * gain_im)
        partial_value = jnp.stack([num_re, num_im, denominator], axis=1)
        summed = lax.psum(partial_value, "col")
        previous = lax.dynamic_slice_in_dim(gain_values, row_at, block_rows, 2)
        gain_block = update_gains(summed, previous)
        gain_values = lax.all_gather(gain_block, "row", axis=2, tiled=True)
    return gain_values


def solution(mesh):
    return jax.shard_map(
        body,
        mesh=mesh,
        in_specs=(
            P(None, "sub", "row", "col"),
            P(None, "sub", "row", "col"),
            P("sub", None),
            P(None, "sub", None),
        ),
        out_specs=P(None, "sub", None),
        check_vma=False,
    )
```

profile of v0, /device:TPU:0, one launch (start us, length us, event | category | flops | bytes accessed | tf_op | source)
XLA Modules:
  0.0 111.2 jit_solution(4182115625880762958)
XLA Ops:
  1.5 6.6 %fusion.25 = f32[8,128,128]{2,1,0:T(8,128)S(1)} fusion(bf16[2,8,128,1024]{3,2,1,0:T(8,128)(2,1)} %param.4, bf16[2,8,128,1024]{3,2,1,0:T(8,128)(2,1)} %param.5, f32[128,128]{1,0:T(8,128)S(1)} %multiply_select_fusion, s32[1024]{0:T(1024)S(1)} %add_select_fusion), kind=kOutput, calls=%fused_computation.26 | convolution fusion | flops 1618214912 | bytes 8982528 | tf_op jit(solution)/shard_map/crk,kq->crq/dot_general | solution.py:24
  8.1 0.9 fusion.61
  9.0 0.9 fusion.59
  10.0 3.0 %fusion.28 = f32[8,128,128]{2,1,0:T(8,128)S(1)} fusion(bf16[2,8,128,1024]{3,2,1,0:T(8,128)(2,1)S(1)} %copy-done.1, bf16[2,8,128,1024]{3,2,1,0:T(8,128)(2,1)S(1)} %copy-done.2, f32[128,128]{1,0:T(8,128)S(1)} %multiply_select_fusion, s32[1024]{0:T(1024)S(1)} %add_select_fusion), kind=kOutput, calls=%fused_computation.27 | convolution fusion | flops 1618214912 | bytes 8982528 | tf_op jit(solution)/shard_map/crk,kq->crq/dot_general | solution.py:24
  13.9 0.9 fusion.58
  14.8 2.7 %fusion.22 = f32[8,128,128]{2,1,0:T(8,128)S(1)} fusion(bf16[2,8,128,1024]{3,2,1,0:T(8,128)(2,1)S(1)} %copy-done.2, f32[128,128]{1,0:T(8,128)S(1)} %multiply_select_fusion, s32[1024]{0:T(1024)S(1)} %add_select_fusion), kind=kOutput, calls=%fused_computation.25 | convolution fusion | flops 1616117760 | bytes 4788224 | tf_op jit(solution)/shard_map/crk,kq->crq/dot_general | solution.py:24
  17.5 0.9 fusion.62
  18.4 20.4 %psum.42 = f32[8,3,128]{2,0,1:T(8,128)S(1)} all-reduce(f32[8,3,128]{2,0,1:T(8,128)S(1)} %pad_maximum_fusion), channel_id=1, replica_groups=mesh['sub'=2,'row'=4,'col'=4] {'col'}, use_global_device_ids=true, to_apply=%region_0.1 | all-reduce | flops 3072 | bytes 24576 | tf_op jit(solution)/shard_map/psum | solution.py:72
  38.9 4.9 %psum.43 = f32[2,128]{1,0:T(2,128)S(1)} all-reduce(f32[2,128]{1,0:T(2,128)S(1)} %broadcast_multiply_fusion.2), channel_id=1, replica_groups=mesh['sub'=2,'row'=4,'col'=4] {'sub'}, use_global_device_ids=true, to_apply=%region_2.3 | all-reduce | flops 256 | bytes 2048 | tf_op jit(solution)/shard_map/psum | solution.py:11
  43.9 5.2 %all_gather.9 = f32[2,8,512]{2,1,0:T(8,128)S(1)} all-gather(f32[2,8,128]{2,1,0:T(8,128)S(1)} %broadcast_add_fusion.2), channel_id=1, replica_groups=mesh['sub'=2,'row'=4,'col'=4] {'row'}, dimensions={2}, use_global_device_ids=true | all-gather | bytes 40960 | tf_op jit(solution)/shard_map/all_gather | solution.py:75
  50.0 0.9 fusion.66
  50.9 0.9 fusion.63
  51.8 0.9 fusion.65
  52.8 0.9 fusion.64
  53.7 15.5 %psum.44 = f32[8,3,128]{2,0,1:T(8,128)S(1)} all-reduce(f32[8,3,128]{2,0,1:T(8,128)S(1)} %pad_maximum_fusion.1), channel_id=1, replica_groups=mesh['sub'=2,'row'=4,'col'=4] {'col'}, use_global_device_ids=true, to_apply=%region_3.4 | all-reduce | flops 3072 | bytes 24576 | tf_op jit(solution)/shard_map/psum | solution.py:72
  69.3 4.9 %psum.45 = f32[2,128]{1,0:T(2,128)S(1)} all-reduce(f32[2,128]{1,0:T(2,128)S(1)} %broadcast_multiply_fusion.1), channel_id=1, replica_groups=mesh['sub'=2,'row'=4,'col'=4] {'sub'}, use_global_device_ids=true, to_apply=%region_5.6 | all-reduce | flops 256 | bytes 2048 | tf_op jit(solution)/shard_map/psum | solution.py:11
  74.3 5.2 %all_gather.10 = f32[2,8,512]{2,1,0:T(8,128)S(1)} all-gather(f32[2,8,128]{2,1,0:T(8,128)S(1)} %broadcast_add_fusion.1), channel_id=1, replica_groups=mesh['sub'=2,'row'=4,'col'=4] {'row'}, dimensions={2}, use_global_device_ids=true | all-gather | bytes 40960 | tf_op jit(solution)/shard_map/all_gather | solution.py:75
  80.4 0.9 fusion.71
  81.3 0.9 fusion.69
  82.2 0.9 fusion.70
  83.2 0.9 fusion.68
  84.1 16.2 %psum.46 = f32[8,3,128]{2,0,1:T(8,128)S(1)} all-reduce(f32[8,3,128]{2,0,1:T(8,128)S(1)} %pad_maximum_fusion.2), channel_id=1, replica_groups=mesh['sub'=2,'row'=4,'col'=4] {'col'}, use_global_device_ids=true, to_apply=%region_6.7 | all-reduce | flops 3072 | bytes 24576 | tf_op jit(solution)/shard_map/psum | solution.py:72
  100.4 4.9 %psum.47 = f32[2,128]{1,0:T(2,128)S(1)} all-reduce(f32[2,128]{1,0:T(2,128)S(1)} %broadcast_multiply_fusion), channel_id=1, replica_groups=mesh['sub'=2,'row'=4,'col'=4] {'sub'}, use_global_device_ids=true, to_apply=%region_8.9 | all-reduce | flops 256 | bytes 2048 | tf_op jit(solution)/shard_map/psum | solution.py:11
  105.3 5.2 %all_gather.11 = f32[2,8,512]{2,1,0:T(8,128)S(1)} all-gather(f32[2,8,128]{2,1,0:T(8,128)S(1)} %broadcast_add_fusion), channel_id=1, replica_groups=mesh['sub'=2,'row'=4,'col'=4] {'row'}, dimensions={2}, use_global_device_ids=true | all-gather | bytes 40960 | tf_op jit(solution)/shard_map/all_gather | solution.py:75
  (42 shorter events, 5.1 us)
Async XLA Ops:
  1.5 8.4 %copy-start.1 = (bf16[2,8,128,1024]{3,2,1,0:T(8,128)(2,1)S(1)}, bf16[2,8,128,1024]{3,2,1,0:T(8,128)(2,1)}, u32[]{:S(2)}) copy-start(bf16[2,8,128,1024]{3,2,1,0:T(8,128)(2,1)} %param.4) | copy-start | bytes 12582916
  1.5 8.4 %copy-start.2 = (bf16[2,8,128,1024]{3,2,1,0:T(8,128)(2,1)S(1)}, bf16[2,8,128,1024]{3,2,1,0:T(8,128)(2,1)}, u32[]{:S(2)}) copy-start(bf16[2,8,128,1024]{3,2,1,0:T(8,128)(2,1)} %param.5) | copy-start | bytes 12582916
  13.9 25.0 %copy-start = (f32[2,8,512]{2,1,0:T(8,128)S(1)}, f32[2,8,512]{2,1,0:T(8,128)}, u32[]{:S(2)}) copy-start(f32[2,8,512]{2,1,0:T(8,128)} %param.7) | copy-start | bytes 98308
where the time goes:
time: 112 us; the launch traced here: 111 us
  blocking collectives  82.5 us (74%)
  matrix products  26.1 us (23%)
  other arithmetic  1.73 us (2%)
    psum x3, blocking collectives, body(): summed = lax.psum(partial_value, 'col')  52.2 us
    all_gather x3, blocking collectives, body(): gain_values = lax.all_gather(gain_block, 'row', axis=2, tiled=True)  15.6 us
    psum x3, blocking collectives, subband_total(): return lax.psum(values, 'sub')  14.8 us
    dot_general x15, matrix products, contract(): jnp.einsum('cpq,cq->cp', matrix, vector, precision=lax.Precision.HIGHEST)  13.9 us
    dot_general x3, matrix products, time_total(): jnp.einsum('crk,kq->crq', values, selector, precision=lax.Precision.HIGHE...  12.3 us

commit v1 on v0

--- a/solution.py
+++ b/solution.py
@@ -5,6 +5,16 @@
 
 TIMES = 8
 ITERS = 3
+
+
+def gather_by_hops(x, axis, along):
+    size = lax.axis_size(axis)
+    held, parts = (x, [x])
+    for _ in range(size - 1):
+        held = lax.ppermute(held, axis, [(i, (i + 1) % size) for i in range(size)])
+        parts.insert(0, held)
+    line = jnp.concatenate(parts, axis=along)
+    return jnp.roll(line, (lax.axis_index(axis) + 1) * x.shape[along], axis=along)
 
 
 def subband_total(values):
@@ -72,7 +82,7 @@
         summed = lax.psum(partial_value, "col")
         previous = lax.dynamic_slice_in_dim(gain_values, row_at, block_rows, 2)
         gain_block = update_gains(summed, previous)
-        gain_values = lax.all_gather(gain_block, "row", axis=2, tiled=True)
+        gain_values = gather_by_hops(gain_block, "row", 2)
     return gain_values
 
 

time: 112 us -> 126 us (1.12)
  waiting for transfers between devices: 0 us -> 27.7 us
  blocking collectives: 82.5 us -> 67 us
  matrix products: 26.1 us -> 28.3 us
    ppermute x0 -> x9, waiting for transfers between devices: none -> 27.7 us  [gather_by_hops(): held = lax.ppermute(held, axis, [(i, (i + 1) % size) for i in range(size)])]
    all_gather x3 -> x0, blocking collectives: 15.6 us -> none  [body(): gain_values = lax.all_gather(gain_block, 'row', axis=2, tiled=True)]
    dot_general x3, matrix products: 12.3 us -> 14.5 us  [time_total(): jnp.einsum('crk,kq->crq', values, selector, precision=lax.Precision.HIGHE...]
  transfers between devices with their start and end apart: 0 -> 9, of which waited for: 0 -> 9; matrix products, arithmetic and copies ran while one was open for 0% -> 0% of each run, Pallas kernels for 0% -> 0%
where the time goes in v1:
time: 126 us
  blocking collectives  67 us (53%)
  matrix products  28.3 us (22%)
  waiting for transfers between devices  27.7 us (22%)
  other arithmetic  2.13 us (2%)
    psum x3, blocking collectives, body(): summed = lax.psum(partial_value, 'col')  52.2 us
    ppermute x9, waiting for transfers between devices, gather_by_hops(): held = lax.ppermute(held, axis, [(i, (i + 1) % size) for i in range(size)])  27.7 us
    psum x3, blocking collectives, subband_total(): return lax.psum(values, 'sub')  14.8 us
    dot_general x3, matrix products, time_total(): jnp.einsum('crk,kq->crq', values, selector, precision=lax.Precision.HIGHE...  14.5 us
    dot_general x15, matrix products, contract(): jnp.einsum('cpq,cq->cp', matrix, vector, precision=lax.Precision.HIGHEST)  13.9 us
  transfers between devices with their start and end apart: 9, of which 9 were waited for; matrix products, arithmetic and copies ran while one was open for 0% of the time, Pallas kernels for 0%

profile of v1, /device:TPU:0, one launch (start us, length us, event | category | flops | bytes accessed | tf_op | source)
XLA Modules:
  0.0 125.6 jit_solution(2977251343283844320)
XLA Ops:
  0.8 6.6 %fusion.25 = f32[8,128,128]{2,1,0:T(8,128)S(1)} fusion(bf16[2,8,128,1024]{3,2,1,0:T(8,128)(2,1)} %param.6, bf16[2,8,128,1024]{3,2,1,0:T(8,128)(2,1)} %param.7, f32[128,128]{1,0:T(8,128)S(1)} %multiply_select_fusion, s32[1024]{0:T(1024)S(1)} %add_select_fusion), kind=kOutput, calls=%fused_computation.26 | convolution fusion | flops 1618214912 | bytes 8982528 | tf_op jit(solution)/shard_map/crk,kq->crq/dot_general | solution.py:34
  7.4 3.0 %fusion.28 = f32[8,128,128]{2,1,0:T(8,128)S(1)} fusion(bf16[2,8,128,1024]{3,2,1,0:T(8,128)(2,1)S(1)} %copy-done.1, bf16[2,8,128,1024]{3,2,1,0:T(8,128)(2,1)S(1)} %copy-done.2, f32[128,128]{1,0:T(8,128)S(1)} %multiply_select_fusion, s32[1024]{0:T(1024)S(1)} %add_select_fusion), kind=kOutput, calls=%fused_computation.27 | convolution fusion | flops 1618214912 | bytes 8982528 | tf_op jit(solution)/shard_map/crk,kq->crq/dot_general | solution.py:34
  11.3 0.9 fusion.66
  12.3 0.9 fusion.67
  14.1 4.9 %fusion.22 = f32[8,128,128]{2,1,0:T(8,128)S(1)} fusion(bf16[2,8,128,1024]{3,2,1,0:T(8,128)(2,1)} %param.7, f32[128,128]{1,0:T(8,128)S(1)} %multiply_select_fusion, s32[1024]{0:T(1024)S(1)} %add_select_fusion), kind=kOutput, calls=%fused_computation.25 | convolution fusion | flops 1616117760 | bytes 4788224 | tf_op jit(solution)/shard_map/crk,kq->crq/dot_general | solution.py:34
  20.0 20.4 %psum.42 = f32[8,3,128]{2,0,1:T(8,128)S(1)} all-reduce(f32[8,3,128]{2,0,1:T(8,128)S(1)} %pad_maximum_fusion), channel_id=1, replica_groups=mesh['sub'=2,'row'=4,'col'=4] {'col'}, use_global_device_ids=true, to_apply=%region_0.1 | all-reduce | flops 3072 | bytes 24576 | tf_op jit(solution)/shard_map/psum | solution.py:82
  40.5 4.9 %psum.43 = f32[2,128]{1,0:T(2,128)S(1)} all-reduce(f32[2,128]{1,0:T(2,128)S(1)} %broadcast_multiply_fusion.2), channel_id=1, replica_groups=mesh['sub'=2,'row'=4,'col'=4] {'sub'}, use_global_device_ids=true, to_apply=%region_2.3 | all-reduce | flops 256 | bytes 2048 | tf_op jit(solution)/shard_map/psum | solution.py:21
  45.7 3.1 %collective-permute-done = f32[2,8,128]{2,1,0:T(8,128)S(1)} collective-permute-done((f32[2,8,128]{2,1,0:T(8,128)S(1)}, f32[2,8,128]{2,1,0:T(8,128)S(1)}, u32[]{:S(2)}, u32[]{:S(2)}) %collective-permute-start) | collective-permute-done | bytes 8224 | tf_op jit(solution)/shard_map/ppermute | solution.py:14
  48.8 3.1 %collective-permute-done.1 = f32[2,8,128]{2,1,0:T(8,128)S(1)} collective-permute-done((f32[2,8,128]{2,1,0:T(8,128)S(1)}, f32[2,8,128]{2,1,0:T(8,128)S(1)}, u32[]{:S(2)}, u32[]{:S(2)}) %collective-permute-start.1) | collective-permute-done | bytes 8224 | tf_op jit(solution)/shard_map/ppermute | solution.py:14
  51.9 3.1 %collective-permute-done.2 = f32[2,8,128]{2,1,0:T(8,128)S(1)} collective-permute-done((f32[2,8,128]{2,1,0:T(8,128)S(1)}, f32[2,8,128]{2,1,0:T(8,128)S(1)}, u32[]{:S(2)}, u32[]{:S(2)}) %collective-permute-start.2) | collective-permute-done | bytes 8224 | tf_op jit(solution)/shard_map/ppermute | solution.py:14
  56.9 0.9 fusion.72
  57.8 0.9 fusion.71
  59.7 15.5 %psum.44 = f32[8,3,128]{2,0,1:T(8,128)S(1)} all-reduce(f32[8,3,128]{2,0,1:T(8,128)S(1)} %pad_maximum_fusion.1), channel_id=1, replica_groups=mesh['sub'=2,'row'=4,'col'=4] {'col'}, use_global_device_ids=true, to_apply=%region_3.5 | all-reduce | flops 3072 | bytes 24576 | tf_op jit(solution)/shard_map/psum | solution.py:82
  75.3 4.9 %psum.45 = f32[2,128]{1,0:T(2,128)S(1)} all-reduce(f32[2,128]{1,0:T(2,128)S(1)} %broadcast_multiply_fusion.1), channel_id=1, replica_groups=mesh['sub'=2,'row'=4,'col'=4] {'sub'}, use_global_device_ids=true, to_apply=%region_5.7 | all-reduce | flops 256 | bytes 2048 | tf_op jit(solution)/shard_map/psum | solution.py:21
  80.4 3.1 %collective-permute-done.3 = f32[2,8,128]{2,1,0:T(8,128)S(1)} collective-permute-done((f32[2,8,128]{2,1,0:T(8,128)S(1)}, f32[2,8,128]{2,1,0:T(8,128)S(1)}, u32[]{:S(2)}, u32[]{:S(2)}) %collective-permute-start.3) | collective-permute-done | bytes 8224 | tf_op jit(solution)/shard_map/ppermute | solution.py:14
  83.4 3.1 %collective-permute-done.4 = f32[2,8,128]{2,1,0:T(8,128)S(1)} collective-permute-done((f32[2,8,128]{2,1,0:T(8,128)S(1)}, f32[2,8,128]{2,1,0:T(8,128)S(1)}, u32[]{:S(2)}, u32[]{:S(2)}) %collective-permute-start.4) | collective-permute-done | bytes 8224 | tf_op jit(solution)/shard_map/ppermute | solution.py:14
  86.5 3.1 %collective-permute-done.5 = f32[2,8,128]{2,1,0:T(8,128)S(1)} collective-permute-done((f32[2,8,128]{2,1,0:T(8,128)S(1)}, f32[2,8,128]{2,1,0:T(8,128)S(1)}, u32[]{:S(2)}, u32[]{:S(2)}) %collective-permute-start.5) | collective-permute-done | bytes 8224 | tf_op jit(solution)/shard_map/ppermute | solution.py:14
  91.5 0.9 fusion.78
  92.4 0.9 fusion.75
  94.3 16.2 %psum.46 = f32[8,3,128]{2,0,1:T(8,128)S(1)} all-reduce(f32[8,3,128]{2,0,1:T(8,128)S(1)} %pad_maximum_fusion.2), channel_id=1, replica_groups=mesh['sub'=2,'row'=4,'col'=4] {'col'}, use_global_device_ids=true, to_apply=%region_6.8 | all-reduce | flops 3072 | bytes 24576 | tf_op jit(solution)/shard_map/psum | solution.py:82
  110.7 4.9 %psum.47 = f32[2,128]{1,0:T(2,128)S(1)} all-reduce(f32[2,128]{1,0:T(2,128)S(1)} %broadcast_multiply_fusion), channel_id=1, replica_groups=mesh['sub'=2,'row'=4,'col'=4] {'sub'}, use_global_device_ids=true, to_apply=%region_8.10 | all-reduce | flops 256 | bytes 2048 | tf_op jit(solution)/shard_map/psum | solution.py:21
  115.7 3.1 %collective-permute-done.6 = f32[2,8,128]{2,1,0:T(8,128)S(1)} collective-permute-done((f32[2,8,128]{2,1,0:T(8,128)S(1)}, f32[2,8,128]{2,1,0:T(8,128)S(1)}, u32[]{:S(2)}, u32[]{:S(2)}) %collective-permute-start.6) | collective-permute-done | bytes 8224 | tf_op jit(solution)/shard_map/ppermute | solution.py:14
  118.8 3.1 %collective-permute-done.7 = f32[2,8,128]{2,1,0:T(8,128)S(1)} collective-permute-done((f32[2,8,128]{2,1,0:T(8,128)S(1)}, f32[2,8,128]{2,1,0:T(8,128)S(1)}, u32[]{:S(2)}, u32[]{:S(2)}) %collective-permute-start.7) | collective-permute-done | bytes 8224 | tf_op jit(solution)/shard_map/ppermute | solution.py:14
  121.8 3.1 %collective-permute-done.8 = f32[2,8,128]{2,1,0:T(8,128)S(1)} collective-permute-done((f32[2,8,128]{2,1,0:T(8,128)S(1)}, f32[2,8,128]{2,1,0:T(8,128)S(1)}, u32[]{:S(2)}, u32[]{:S(2)}) %collective-permute-start.8) | collective-permute-done | bytes 8224 | tf_op jit(solution)/shard_map/ppermute | solution.py:14
  (59 shorter events, 10.7 us)
Async XLA Ops:
  0.8 6.6 %copy-start.1 = (bf16[2,8,128,1024]{3,2,1,0:T(8,128)(2,1)S(1)}, bf16[2,8,128,1024]{3,2,1,0:T(8,128)(2,1)}, u32[]{:S(2)}) copy-start(bf16[2,8,128,1024]{3,2,1,0:T(8,128)(2,1)} %param.6) | copy-start | bytes 12582916
  0.8 6.6 %copy-start.2 = (bf16[2,8,128,1024]{3,2,1,0:T(8,128)(2,1)S(1)}, bf16[2,8,128,1024]{3,2,1,0:T(8,128)(2,1)}, u32[]{:S(2)}) copy-start(bf16[2,8,128,1024]{3,2,1,0:T(8,128)(2,1)} %param.7) | copy-start | bytes 12582916
  7.4 3.0 %copy-start = (f32[2,8,512]{2,1,0:T(8,128)S(1)}, f32[2,8,512]{2,1,0:T(8,128)}, u32[]{:S(2)}) copy-start(f32[2,8,512]{2,1,0:T(8,128)} %param.9) | copy-start | bytes 98308
  45.5 3.3 %collective-permute-start = (f32[2,8,128]{2,1,0:T(8,128)S(1)}, f32[2,8,128]{2,1,0:T(8,128)S(1)}, u32[]{:S(2)}, u32[]{:S(2)}) collective-permute-start(f32[2,8,128]{2,1,0:T(8,128)S(1)} %broadcast_add_fusion.2), channel_id=1, source_target_pairs={{0,4},{4,8},{8,12},{12,0},{1,5},{5,9},{9,13},{13,1},{2,6},{6,10},{... | collective-permute-start | bytes 24584 | tf_op jit(solution)/shard_map/ppermute | solution.py:14
  48.8 3.1 %collective-permute-start.1 = (f32[2,8,128]{2,1,0:T(8,128)S(1)}, f32[2,8,128]{2,1,0:T(8,128)S(1)}, u32[]{:S(2)}, u32[]{:S(2)}) collective-permute-start(f32[2,8,128]{2,1,0:T(8,128)S(1)} %collective-permute-done), channel_id=1, source_target_pairs={{0,4},{4,8},{8,12},{12,0},{1,5},{5,9},{9,13},{13,1},{2,6},{6,10},{... | collective-permute-start | bytes 24584 | tf_op jit(solution)/shard_map/ppermute | solution.py:14
  51.9 3.1 %collective-permute-start.2 = (f32[2,8,128]{2,1,0:T(8,128)S(1)}, f32[2,8,128]{2,1,0:T(8,128)S(1)}, u32[]{:S(2)}, u32[]{:S(2)}) collective-permute-start(f32[2,8,128]{2,1,0:T(8,128)S(1)} %collective-permute-done.1), channel_id=1, source_target_pairs={{0,4},{4,8},{8,12},{12,0},{1,5},{5,9},{9,13},{13,1},{2,6},{6,10},{... | collective-permute-start | bytes 24584 | tf_op jit(solution)/shard_map/ppermute | solution.py:14
  80.3 3.1 %collective-permute-start.3 = (f32[2,8,128]{2,1,0:T(8,128)S(1)}, f32[2,8,128]{2,1,0:T(8,128)S(1)}, u32[]{:S(2)}, u32[]{:S(2)}) collective-permute-start(f32[2,8,128]{2,1,0:T(8,128)S(1)} %broadcast_add_fusion.1), channel_id=1, source_target_pairs={{0,4},{4,8},{8,12},{12,0},{1,5},{5,9},{9,13},{13,1},{2,6},{6,10},{... | collective-permute-start | bytes 24584 | tf_op jit(solution)/shard_map/ppermute | solution.py:14
  83.4 3.1 %collective-permute-start.4 = (f32[2,8,128]{2,1,0:T(8,128)S(1)}, f32[2,8,128]{2,1,0:T(8,128)S(1)}, u32[]{:S(2)}, u32[]{:S(2)}) collective-permute-start(f32[2,8,128]{2,1,0:T(8,128)S(1)} %collective-permute-done.3), channel_id=1, source_target_pairs={{0,4},{4,8},{8,12},{12,0},{1,5},{5,9},{9,13},{13,1},{2,6},{6,10},{... | collective-permute-start | bytes 24584 | tf_op jit(solution)/shard_map/ppermute | solution.py:14
  86.5 3.1 %collective-permute-start.5 = (f32[2,8,128]{2,1,0:T(8,128)S(1)}, f32[2,8,128]{2,1,0:T(8,128)S(1)}, u32[]{:S(2)}, u32[]{:S(2)}) collective-permute-start(f32[2,8,128]{2,1,0:T(8,128)S(1)} %collective-permute-done.4), channel_id=1, source_target_pairs={{0,4},{4,8},{8,12},{12,0},{1,5},{5,9},{9,13},{13,1},{2,6},{6,10},{... | collective-permute-start | bytes 24584 | tf_op jit(solution)/shard_map/ppermute | solution.py:14
  115.7 3.1 %collective-permute-start.6 = (f32[2,8,128]{2,1,0:T(8,128)S(1)}, f32[2,8,128]{2,1,0:T(8,128)S(1)}, u32[]{:S(2)}, u32[]{:S(2)}) collective-permute-start(f32[2,8,128]{2,1,0:T(8,128)S(1)} %broadcast_add_fusion), channel_id=1, source_target_pairs={{0,4},{4,8},{8,12},{12,0},{1,5},{5,9},{9,13},{13,1},{2,6},{6,10},{... | collective-permute-start | bytes 24584 | tf_op jit(solution)/shard_map/ppermute | solution.py:14
  118.8 3.1 %collective-permute-start.7 = (f32[2,8,128]{2,1,0:T(8,128)S(1)}, f32[2,8,128]{2,1,0:T(8,128)S(1)}, u32[]{:S(2)}, u32[]{:S(2)}) collective-permute-start(f32[2,8,128]{2,1,0:T(8,128)S(1)} %collective-permute-done.6), channel_id=1, source_target_pairs={{0,4},{4,8},{8,12},{12,0},{1,5},{5,9},{9,13},{13,1},{2,6},{6,10},{... | collective-permute-start | bytes 24584 | tf_op jit(solution)/shard_map/ppermute | solution.py:14
  121.8 3.1 %collective-permute-start.8 = (f32[2,8,128]{2,1,0:T(8,128)S(1)}, f32[2,8,128]{2,1,0:T(8,128)S(1)}, u32[]{:S(2)}, u32[]{:S(2)}) collective-permute-start(f32[2,8,128]{2,1,0:T(8,128)S(1)} %collective-permute-done.7), channel_id=1, source_target_pairs={{0,4},{4,8},{8,12},{12,0},{1,5},{5,9},{9,13},{13,1},{2,6},{6,10},{... | collective-permute-start | bytes 24584 | tf_op jit(solution)/shard_map/ppermute | solution.py:14
